TPU v7x, 512 devices: a whole 4x8x8 slice. The times are simulated.
512 devices in a mesh: slab: 128 (over x_lo, z, y), band: 4 (over x_hi, core).
Axes of the slice: x: 4 (x_hi: 2, x_lo: 2; x = x_hi * 2 + x_lo), y: 8, z: 8, core: 2. Of those that a mesh axis runs over, the one named last changes fastest.
Arguments:
- orbitals: float32 [8, 128, 128, 128], P('band', 'slab'), may hold values from -6 to 6
Outputs:
- exchange_out: float32 [8, 128, 128, 128], P('band', 'slab')
All inputs are finite; a program needn't handle non-finite values.
Results may differ from a plain program's by a relative error of at most 0.00013.
Values sent between devices are 32-bit elements; how exact they have to be, the bound alone decides.
A program may use at most 64 MiB of HBM per device.

v0:
```python
import math

import jax
import jax.numpy as jnp
from jax import lax
from jax.sharding import PartitionSpec as P

screen_width = 0.5
highest = lax.Precision.HIGHEST


def shifted(value, axis, steps):
    count = lax.axis_size(axis)
    pairs = [(source, (source + steps) % count) for source in range(count)]
    return lax.ppermute(value, axis, pairs)


def dft_tables(length):
    counter = jnp.arange(length, dtype=jnp.int32)
    product = counter[:, None] * counter[None, :] % length
    angles = 2.0 * math.pi / length * product.astype(jnp.float32)
    return (jnp.cos(angles), jnp.sin(angles))


def frequency(counter, length):
    return jnp.where(counter < length // 2, counter, counter - length).astype(jnp.float32)


def screened(squared):
    safe_sq = jnp.where(squared > 0, squared, 1.0)
    value = 4.0 * math.pi / safe_sq * (1.0 - jnp.exp(-safe_sq / (4.0 * screen_width**2)))
    return jnp.where(squared > 0, value, math.pi / screen_width**2)


def rotate(real_part, imag_part, cosine, sine_table, form, forward):
    sign = 1.0 if forward else -1.0
    real_cos = jnp.einsum(form, real_part, cosine, precision=highest)
    imag_sin = jnp.einsum(form, imag_part, sine_table, precision=highest)
    imag_cos = jnp.einsum(form, imag_part, cosine, precision=highest)
    real_sin = jnp.einsum(form, real_part, sine_table, precision=highest)
    return (real_cos + sign * imag_sin, imag_cos - sign * real_sin)


def potentials(density):
    count, planes, rows, columns = density.shape
    depth = planes * lax.axis_size("slab")
    cos_x, sin_x = dft_tables(columns)
    cos_y, sin_y = dft_tables(rows)
    cos_z, sin_z = dft_tables(depth)
    form_x = "pzyx,xk->pzyk"
    first = density[0::2]
    second = density[1::2]
    real_part = jnp.einsum(form_x, first, cos_x, precision=highest) + jnp.einsum(
        form_x, second, sin_x, precision=highest
    )
    imag_part = jnp.einsum(form_x, second, cos_x, precision=highest) - jnp.einsum(
        form_x, first, sin_x, precision=highest
    )
    real_part, imag_part = rotate(real_part, imag_part, cos_y, sin_y, "pzyx,yk->pzkx", True)
    part_re = lax.all_to_all(real_part, "slab", split_axis=2, concat_axis=1, tiled=True)
    part_im = lax.all_to_all(imag_part, "slab", split_axis=2, concat_axis=1, tiled=True)
    band_rows = part_re.shape[2]
    row_index = lax.axis_index("slab") * band_rows + jnp.arange(band_rows, dtype=jnp.int32)
    freq_z = frequency(jnp.arange(depth, dtype=jnp.int32), depth)
    freq_y = frequency(row_index, rows)
    freq_x = frequency(jnp.arange(columns, dtype=jnp.int32), columns)
    squared = ((2.0 * math.pi / depth * freq_z) ** 2)[:, None, None]
    squared = squared + ((2.0 * math.pi / rows * freq_y) ** 2)[None, :, None]
    squared = squared + ((2.0 * math.pi / columns * freq_x) ** 2)[None, None, :]
    weight = screened(squared)
    part_re, part_im = rotate(part_re, part_im, cos_z, sin_z, "pzyx,zk->pkyx", True)
    part_re = part_re * weight
    part_im = part_im * weight
    part_re, part_im = rotate(part_re, part_im, cos_z, sin_z, "pzyx,zk->pkyx", False)
    real_part = lax.all_to_all(part_re, "slab", split_axis=1, concat_axis=2, tiled=True)
    imag_part = lax.all_to_all(part_im, "slab", split_axis=1, concat_axis=2, tiled=True)
    real_part, imag_part = rotate(real_part, imag_part, cos_y, sin_y, "pzyx,yk->pzkx", False)
    factor = 1.0 / (columns * rows * depth)
    real_out = jnp.einsum(form_x, real_part, cos_x, precision=highest) - jnp.einsum(
        form_x, imag_part, sin_x, precision=highest
    )
    imag_out = jnp.einsum(form_x, imag_part, cos_x, precision=highest) + jnp.einsum(
        form_x, real_part, sin_x, precision=highest
    )
    stacked = jnp.stack([real_out * factor, imag_out * factor], axis=1)
    return stacked.reshape(count, planes, rows, columns)


def body(orbitals):
    count = orbitals.shape[0]
    grid_shape = orbitals.shape[1:]
    neighbour = shifted(orbitals, "band", 1)
    result = jnp.zeros_like(orbitals)
    partners = jnp.concatenate([orbitals, neighbour], axis=0)
    width = partners.shape[0]
    density = (orbitals[:, None] * partners[None, :]).reshape((count * width,) + grid_shape)
    field = potentials(density).reshape((count, width) + grid_shape)
    result = result - jnp.sum(field * partners[None], axis=1)
    return result


def solution(mesh):
    placed = (P("band", "slab", None, None),)
    return jax.shard_map(
        body, mesh=mesh, in_specs=placed, out_specs=P("band", "slab", None, None), check_vma=False
    )
```

profile of v0, /device:TPU:4, one launch (start us, length us, event | category | flops | bytes accessed | tf_op | source)
XLA Modules:
  0.0 118.4 jit_solution(16676148683064051228)
XLA Ops:
  0.0 0.0 copy-start
  0.0 2.0 %collective-permute-start = (f32[2,1,128,128]{3,2,1,0:T(8,128)}, f32[2,1,128,128]{3,2,1,0:T(8,128)S(1)}, u32[]{:S(2)}, u32[]{:S(2)}) collective-permute-start(f32[2,1,128,128]{3,2,1,0:T(8,128)} %param.1), channel_id=1, source_target_pairs={{0,1},{1,2},{2,3},{3,0},{4,5},{5,6},{6,7},{7,4},{8,9},{9,10},{10,1... | collective-permute-start | bytes 393224 | tf_op jit(solution)/shard_map/ppermute | solution.py:15
  2.0 6.1 %collective-permute-done = f32[2,1,128,128]{3,2,1,0:T(8,128)S(1)} collective-permute-done((f32[2,1,128,128]{3,2,1,0:T(8,128)}, f32[2,1,128,128]{3,2,1,0:T(8,128)S(1)}, u32[]{:S(2)}, u32[]{:S(2)}) %collective-permute-start) | collective-permute-done | bytes 131104 | tf_op jit(solution)/shard_map/ppermute | solution.py:15
  8.1 0.9 maximum_bitcast_fusion
  9.1 0.0 copy-done
  9.1 0.6 fusion.33
  9.7 0.6 fusion.37
  10.3 0.6 convolution_subtract_fusion.3
  11.0 0.7 fusion.76
  11.6 0.6 convolution_add_fusion.3
  12.3 0.7 fusion.14
  12.9 0.9 copy.67
  13.8 18.4 %all-to-all-start.1 = ((f32[4,1,128,128]{3,0,1,2:T(4,128)}), f32[4,1,128,128]{3,0,1,2:T(4,128)S(1)}, u32[]{:S(2)}, u32[]{:S(2)}) async-start(f32[4,1,128,128]{3,0,1,2:T(4,128)} %copy.67), calls=%async_computation.1 | async-start | bytes 524288 | tf_op jit(solution)/shard_map/all_to_all | solution.py:61
  32.2 0.7 fusion.84
  32.9 0.7 fusion.15
  33.6 0.9 copy.62
  34.4 12.4 %all-to-all-done.1 = f32[4,1,128,128]{3,0,1,2:T(4,128)S(1)} async-done(((f32[4,1,128,128]{3,0,1,2:T(4,128)}), f32[4,1,128,128]{3,0,1,2:T(4,128)S(1)}, u32[]{:S(2)}, u32[]{:S(2)}) %all-to-all-start.1) | async-done | bytes 262176 | tf_op jit(solution)/shard_map/all_to_all | solution.py:61
  46.8 6.3 %all-to-all-start = ((f32[4,1,128,128]{3,0,1,2:T(4,128)}), f32[4,1,128,128]{3,0,1,2:T(4,128)S(1)}, u32[]{:S(2)}, u32[]{:S(2)}) async-start(f32[4,1,128,128]{3,0,1,2:T(4,128)} %copy.62), calls=%async_computation | async-start | bytes 524288 | tf_op jit(solution)/shard_map/all_to_all | solution.py:60
  53.2 0.1 fusion.53
  53.3 0.7 fusion.27
  53.9 13.6 %all-to-all-done = f32[4,1,128,128]{3,0,1,2:T(4,128)S(1)} async-done(((f32[4,1,128,128]{3,0,1,2:T(4,128)}), f32[4,1,128,128]{3,0,1,2:T(4,128)S(1)}, u32[]{:S(2)}, u32[]{:S(2)}) %all-to-all-start) | async-done | bytes 262176 | tf_op jit(solution)/shard_map/all_to_all | solution.py:60
  67.5 0.7 fusion.19
  68.2 0.7 fusion.73
  68.8 0.7 fusion.31
  69.5 0.7 fusion.17
  70.1 0.7 fusion.9
  70.8 0.9 copy.79
  71.7 6.2 %all-to-all-start.3 = ((f32[4,128,1,128]{3,0,2,1:T(4,128)}), f32[4,128,1,128]{3,0,2,1:T(4,128)S(1)}, u32[]{:S(2)}, u32[]{:S(2)}) async-start(f32[4,128,1,128]{3,0,2,1:T(4,128)} %copy.79), calls=%async_computation.3 | async-start | bytes 524288 | tf_op jit(solution)/shard_map/all_to_all | solution.py:76
  77.9 0.6 fusion.87
  78.5 0.7 fusion.11
  79.2 0.9 copy.74
  80.1 12.3 %all-to-all-done.3 = f32[4,128,1,128]{3,0,2,1:T(4,128)S(1)} async-done(((f32[4,128,1,128]{3,0,2,1:T(4,128)}), f32[4,128,1,128]{3,0,2,1:T(4,128)S(1)}, u32[]{:S(2)}, u32[]{:S(2)}) %all-to-all-start.3) | async-done | bytes 262176 | tf_op jit(solution)/shard_map/all_to_all | solution.py:76
  92.4 6.4 %all-to-all-start.2 = ((f32[4,128,1,128]{3,0,2,1:T(4,128)}), f32[4,128,1,128]{3,0,2,1:T(4,128)S(1)}, u32[]{:S(2)}, u32[]{:S(2)}) async-start(f32[4,128,1,128]{3,0,2,1:T(4,128)} %copy.74), calls=%async_computation.2 | async-start | bytes 524288 | tf_op jit(solution)/shard_map/all_to_all | solution.py:75
  98.8 0.7 fusion.21
  99.4 13.7 %all-to-all-done.2 = f32[4,128,1,128]{3,0,2,1:T(4,128)S(1)} async-done(((f32[4,128,1,128]{3,0,2,1:T(4,128)}), f32[4,128,1,128]{3,0,2,1:T(4,128)S(1)}, u32[]{:S(2)}, u32[]{:S(2)}) %all-to-all-start.2) | async-done | bytes 262176 | tf_op jit(solution)/shard_map/all_to_all | solution.py:75
  113.1 0.7 fusion.5
  113.8 0.6 fusion.78
  114.4 0.7 fusion.25
  115.0 0.7 fusion.7
  115.7 0.6 fusion.80
  116.3 0.6 fusion.1
  116.9 0.6 fusion.3
  117.6 0.1 fusion.20
  117.7 0.7 subtract_bitcast_fusion
  (4 shorter events, 0.1 us)
Async XLA Ops:
  0.0 9.1 %copy-start = (f32[2,1,128,128]{3,2,1,0:T(8,128)S(1)}, f32[2,1,128,128]{3,2,1,0:T(8,128)}, u32[]{:S(2)}) copy-start(f32[2,1,128,128]{3,2,1,0:T(8,128)} %param.1) | copy-start | bytes 393220
  0.0 8.1 %collective-permute-start = (f32[2,1,128,128]{3,2,1,0:T(8,128)}, f32[2,1,128,128]{3,2,1,0:T(8,128)S(1)}, u32[]{:S(2)}, u32[]{:S(2)}) collective-permute-start(f32[2,1,128,128]{3,2,1,0:T(8,128)} %param.1), channel_id=1, source_target_pairs={{0,1},{1,2},{2,3},{3,0},{4,5},{5,6},{6,7},{7,4},{8,9},{9,10},{10,1... | collective-permute-start | bytes 393224 | tf_op jit(solution)/shard_map/ppermute | solution.py:15
  13.8 33.0 %all-to-all-start.1 = ((f32[4,1,128,128]{3,0,1,2:T(4,128)}), f32[4,1,128,128]{3,0,1,2:T(4,128)S(1)}, u32[]{:S(2)}, u32[]{:S(2)}) async-start(f32[4,1,128,128]{3,0,1,2:T(4,128)} %copy.67), calls=%async_computation.1 | async-start | bytes 524288 | tf_op jit(solution)/shard_map/all_to_all | solution.py:61
  46.8 20.7 %all-to-all-start = ((f32[4,1,128,128]{3,0,1,2:T(4,128)}), f32[4,1,128,128]{3,0,1,2:T(4,128)S(1)}, u32[]{:S(2)}, u32[]{:S(2)}) async-start(f32[4,1,128,128]{3,0,1,2:T(4,128)} %copy.62), calls=%async_computation | async-start | bytes 524288 | tf_op jit(solution)/shard_map/all_to_all | solution.py:60
  71.7 20.7 %all-to-all-start.3 = ((f32[4,128,1,128]{3,0,2,1:T(4,128)}), f32[4,128,1,128]{3,0,2,1:T(4,128)S(1)}, u32[]{:S(2)}, u32[]{:S(2)}) async-start(f32[4,128,1,128]{3,0,2,1:T(4,128)} %copy.79), calls=%async_computation.3 | async-start | bytes 524288 | tf_op jit(solution)/shard_map/all_to_all | solution.py:76
  92.4 20.7 %all-to-all-start.2 = ((f32[4,128,1,128]{3,0,2,1:T(4,128)}), f32[4,128,1,128]{3,0,2,1:T(4,128)S(1)}, u32[]{:S(2)}, u32[]{:S(2)}) async-start(f32[4,128,1,128]{3,0,2,1:T(4,128)} %copy.74), calls=%async_computation.2 | async-start | bytes 524288 | tf_op jit(solution)/shard_map/all_to_all | solution.py:75
where the time goes:
time: 119 us; the launch traced here: 118 us
  waiting for transfers between devices  58 us (49%)
  starting transfers between devices  39.3 us (33%)
  matrix products  15.4 us (13%)
  local copies, waits for them, and re-layouts  3.51 us (3%)
  other arithmetic  1.82 us (2%)
    all_to_all x1, starting transfers between devices, potentials(): lax.all_to_all(imag_part, 'slab', split_axis=2, concat_axis=1, tiled=True)  18.4 us
    all_to_all x1, waiting for transfers between devices, potentials(): lax.all_to_all(part_re, 'slab', split_axis=1, concat_axis=2, tiled=True)  13.7 us
    all_to_all x1, waiting for transfers between devices, potentials(): lax.all_to_all(real_part, 'slab', split_axis=2, concat_axis=1, tiled=True)  13.6 us
    all_to_all x1, waiting for transfers between devices, potentials(): lax.all_to_all(imag_part, 'slab', split_axis=2, concat_axis=1, tiled=True)  12.4 us
    all_to_all x1, waiting for transfers between devices, potentials(): lax.all_to_all(part_im, 'slab', split_axis=1, concat_axis=2, tiled=True)  12.3 us
    all_to_all x1, starting transfers between devices, potentials(): lax.all_to_all(part_re, 'slab', split_axis=1, concat_axis=2, tiled=True)  6.37 us
    all_to_all x1, starting transfers between devices, potentials(): lax.all_to_all(real_part, 'slab', split_axis=2, concat_axis=1, tiled=True)  6.33 us
    all_to_all x1, starting transfers between devices, potentials(): lax.all_to_all(part_im, 'slab', split_axis=1, concat_axis=2, tiled=True)  6.17 us
  transfers between devices with their start and end apart: 5, of which 5 were waited for; matrix products, arithmetic and copies ran while one was open for 5% of the time, Pallas kernels for 0%

commit v1 on v0

v1 whole, which is shorter than its diff:
```python
import functools
import math

import jax
import jax.numpy as jnp
import numpy as np
from jax import lax
from jax.experimental import pallas as pl
from jax.experimental.pallas import tpu as pltpu
from jax.sharding import PartitionSpec as P

screen_width = 0.5
N = 128
BANDS = 4
LOGICAL = pl.DeviceIdType.LOGICAL
CHUNKS = ((0, 3), (3, 4))


def basis():
    row = np.arange(N)
    freq = np.where(row <= N // 2, row, row - N // 2)
    angle = 2.0 * np.pi / N * ((freq[:, None] * row[None, :]) % N)
    table = np.where(row[:, None] <= N // 2, np.cos(angle), np.sin(angle)) * np.sqrt(2.0 / N)
    table[0] *= np.sqrt(0.5)
    table[N // 2] *= np.sqrt(0.5)
    high = table.astype(np.float32).astype(jnp.bfloat16)
    low = (table - high.astype(np.float64)).astype(np.float32).astype(jnp.bfloat16)
    return np.stack([high, low, high.T, low.T])


def offsets():
    ring = lambda d: min(d, 8 - d)
    steps = [(dx, dz, dy) for dx in range(2) for dz in range(8) for dy in range(8)]
    steps.remove((0, 0, 0))
    return sorted(steps, key=lambda s: -(s[0] + ring(s[1]) + ring(s[2])))


def split(value):
    high = value.astype(jnp.bfloat16)
    return high, (value - high.astype(jnp.float32)).astype(jnp.bfloat16)


def times(value, right):
    both = jnp.dot(jnp.concatenate(split(value), axis=1), right, preferred_element_type=jnp.float32)
    return both[:, :N] + both[:, N:]


def applied(left, value):
    both = jnp.dot(left, jnp.concatenate(split(value), axis=0), preferred_element_type=jnp.float32)
    return both[:N] + both[N:]


def screened(squared):
    safe_sq = jnp.where(squared > 0, squared, 1.0)
    value = 4.0 * math.pi / safe_sq * (1.0 - jnp.exp(-safe_sq / (4.0 * screen_width**2)))
    return jnp.where(squared > 0, value, math.pi / screen_width**2)


def squares(index):
    freq = jnp.where(index <= N // 2, index, index - N // 2).astype(jnp.float32)
    return (2.0 * math.pi / N * freq) ** 2


def kernel(
    orb_hbm, basis_hbm, out_ref, own, other, tables, out1, in1, out2, in2, weight,
    load_sem, near_send, near_recv, send_sem, recv_sem,
):
    me, band = lax.axis_index("slab"), lax.axis_index("band")
    x, z, y = lax.div(me, 64), lax.rem(lax.div(me, 8), 8), lax.rem(me, 8)
    at_x = [lax.rem(x + d, 2) * (64 * BANDS) + band for d in range(2)]
    at_z = [lax.rem(z + d, 8) * (8 * BANDS) for d in range(8)]
    at_y = [lax.rem(y + d, 8) * BANDS for d in range(8)]
    peers = [(lax.rem(x + dx, 2) * 64 + lax.rem(z + dz, 8) * 8 + lax.rem(y + dy, 8), at_x[dx] + at_z[dz] + at_y[dy]) for dx, dz, dy in offsets()]
    following = me * BANDS + lax.rem(band + 1, BANDS)
    previous = me * BANDS + lax.rem(band + BANDS - 1, BANDS)

    load_own = pltpu.make_async_copy(orb_hbm, own, load_sem.at[0])
    load_tables = pltpu.make_async_copy(basis_hbm, tables, load_sem.at[1])
    load_own.start()
    load_tables.start()

    barrier = pltpu.get_barrier_semaphore()
    for _, device in peers:
        pl.semaphore_signal(barrier, inc=1, device_id=device, device_id_type=LOGICAL)
    pl.semaphore_signal(barrier, inc=1, device_id=previous, device_id_type=LOGICAL)

    def sends(source, target, number):
        first, rows = CHUNKS[number % 2]
        for slab, device in peers:
            pltpu.make_async_remote_copy(
                src_ref=source.at[slab, pl.ds(first, rows)],
                dst_ref=target.at[me, pl.ds(first, rows)],
                send_sem=send_sem.at[number],
                recv_sem=recv_sem.at[number],
                device_id=device,
                device_id_type=LOGICAL,
            ).start()
        target[me, pl.ds(first, rows)] = source[me, pl.ds(first, rows)]

    def whole(source, target, number):
        first, rows = CHUNKS[number % 2]
        return pltpu.make_async_remote_copy(
            src_ref=source.at[pl.ds(0, N - 1), pl.ds(first, rows)],
            dst_ref=target.at[pl.ds(0, N - 1), pl.ds(first, rows)],
            send_sem=send_sem.at[number],
            recv_sem=recv_sem.at[number],
            device_id=following,
            device_id_type=LOGICAL,
        )

    def gather(ref, chunk):
        first, rows = CHUNKS[chunk]
        flat = ref.reshape(N * 8, N)
        return jnp.concatenate([flat[pl.ds(first + p, N, stride=8), :] for p in range(rows)], axis=1)

    def scatter(ref, chunk, value):
        first, rows = CHUNKS[chunk]
        flat = ref.reshape(N * 8, N)
        for p in range(rows):
            flat[pl.ds(first + p, N, stride=8), :] = value[:, p * N : (p + 1) * N]

    row = lax.broadcasted_iota(jnp.int32, (N, N), 0)
    column = lax.broadcasted_iota(jnp.int32, (N, N), 1)
    weight[...] = screened(squares(row) + squares(jnp.full((N, N), me, jnp.int32)) + squares(column))

    load_own.wait()
    load_tables.wait()
    high, low, high_t, low_t = (tables[i] for i in range(4))

    def right_of(a, b):
        both = jnp.concatenate([a, b], axis=1)
        return jnp.concatenate([both, both], axis=0)

    def left_of(a, b):
        both = jnp.concatenate([a, b], axis=0)
        return jnp.concatenate([both, both], axis=1)

    def forward(chunk, densities):
        first = times(jnp.concatenate(densities, axis=0), right_of(high_t, low_t))
        side = jnp.concatenate([first[p * N : (p + 1) * N] for p in range(len(densities))], axis=1)
        scatter(out1, chunk, applied(left_of(high, low), side))

    def middle(chunk):
        spectrum = applied(left_of(high, low), gather(in1, chunk))
        spectrum = spectrum * jnp.concatenate([weight[...]] * CHUNKS[chunk][1], axis=1)
        scatter(out2, chunk, applied(left_of(high_t, low_t), spectrum))

    def backward(chunk):
        rows = CHUNKS[chunk][1]
        side = applied(left_of(high_t, low_t), gather(in2, chunk))
        stack = jnp.concatenate([side[:, p * N : (p + 1) * N] for p in range(rows)], axis=0)
        field = times(stack, right_of(high, low))
        return [field[p * N : (p + 1) * N] for p in range(rows)]

    forward(0, [own[0] * own[0], own[0] * own[1], own[1] * own[1]])

    pl.semaphore_wait(barrier, N)
    shift = pltpu.make_async_remote_copy(
        src_ref=own, dst_ref=other, send_sem=near_send, recv_sem=near_recv, device_id=following, device_id_type=LOGICAL
    )
    shift.start()
    sends(out1, in1, 0)
    shift.wait_recv()
    forward(1, [own[0] * other[0], own[0] * other[1], own[1] * other[0], own[1] * other[1]])
    sends(out1, in1, 1)
    for chunk in range(2):
        whole(out1, in1, chunk).wait_recv()
        middle(chunk)
        sends(out2, in2, 2 + chunk)
    whole(out2, in2, 2).wait_recv()
    field = backward(0)
    own_part = [field[0] * own[0] + field[1] * own[1], field[1] * own[0] + field[2] * own[1]]
    whole(out2, in2, 3).wait_recv()
    field = backward(1)
    out_ref[0] = -(own_part[0] + (field[0] * other[0] + field[1] * other[1]))
    out_ref[1] = -(own_part[1] + (field[2] * other[0] + field[3] * other[1]))
    shift.wait_send()
    for number in range(4):
        source, target = ((out1, in1), (out2, in2))[number // 2]
        whole(source, target, number).wait_send()


def body(orbitals):
    plane = pltpu.VMEM((N, 8, N), jnp.float32)
    pair = pltpu.VMEM((2, N, N), jnp.float32)
    result = pl.pallas_call(
        kernel,
        out_shape=jax.ShapeDtypeStruct((2, N, N), jnp.float32),
        in_specs=[pl.BlockSpec(memory_space=pl.ANY)] * 2,
        out_specs=pl.BlockSpec(memory_space=pltpu.VMEM),
        scratch_shapes=[
            pair,
            pair,
            pltpu.VMEM((4, N, N), jnp.bfloat16),
            plane,
            plane,
            plane,
            plane,
            pltpu.VMEM((N, N), jnp.float32),
            pltpu.SemaphoreType.DMA((2,)),
            pltpu.SemaphoreType.DMA,
            pltpu.SemaphoreType.DMA,
            pltpu.SemaphoreType.DMA((4,)),
            pltpu.SemaphoreType.DMA((4,)),
        ],
        compiler_params=pltpu.CompilerParams(collective_id=0, has_side_effects=True),
        name="exchange",
    )(orbitals.reshape(2, N, N), jnp.asarray(basis()))
    return result.reshape(orbitals.shape)


def solution(mesh):
    placed = P("band", "slab", None, None)
    return jax.shard_map(body, mesh=mesh, in_specs=(placed,), out_specs=placed, check_vma=False)
```

time: 119 us -> 43.9 us (0.37)
  the two profiles are of different devices: /device:TPU:4 before, /device:TPU:12 now
where the time goes in v1:
time: 43.9 us; the launch traced here: 43.8 us
  Pallas kernels  42.2 us (96%)
  local copies, waits for them, and re-layouts  1.57 us (4%)
    pallas_call x1, Pallas kernels, body(): pl.pallas_call(kernel, out_shape=jax.ShapeDtypeStruct((2, N, N), jnp.floa...  42.2 us
    unnamed x1, local copies, waits for them, and re-layouts  1.57 us

profile of v1, /device:TPU:12, one launch (start us, length us, event | category | flops | bytes accessed | tf_op | source)
XLA Modules:
  0.0 43.8 jit_solution(6663540236881270508)
XLA Ops:
  0.0 42.2 %exchange.1 = f32[2,128,128]{2,1,0:T(8,128)} custom-call(f32[2,128,128]{2,1,0:T(8,128)} %bitcast.5, bf16[4,128,128]{2,1,0:T(8,128)(2,1)} %constant.2.clone.basis_hbm), custom_call_target="tpu_custom_call" | custom-call | tf_op jit(solution)/shard_map/exchange/pallas_call | solution.py:186
  42.2 1.6 %copy.5 = f32[2,1,128,128]{3,2,1,0:T(8,128)} copy(f32[2,1,128,128]{3,2,1,0:T(8,128)} %bitcast.4) | data formatting | bytes 262144

commit v2 on v1

--- a/solution.py
+++ b/solution.py
@@ -35,6 +35,12 @@
     return sorted(steps, key=lambda s: -(s[0] + ring(s[1]) + ring(s[2])))
 
 
+def plane_offsets():
+    ring = lambda d: min(d, 8 - d)
+    steps = [(dx, dy) for dx in range(2) for dy in range(8)]
+    return sorted(steps, key=lambda s: -(s[0] + ring(s[1])))
+
+
 def split(value):
     high = value.astype(jnp.bfloat16)
     return high, (value - high.astype(jnp.float32)).astype(jnp.bfloat16)
@@ -65,6 +71,10 @@
     orb_hbm, basis_hbm, out_ref, own, other, tables, out1, in1, out2, in2, weight,
     load_sem, near_send, near_recv, send_sem, recv_sem,
 ):
+    load_own = pltpu.make_async_copy(orb_hbm, own, load_sem.at[0])
+    load_tables = pltpu.make_async_copy(basis_hbm, tables, load_sem.at[1])
+    load_own.start()
+    load_tables.start()
     me, band = lax.axis_index("slab"), lax.axis_index("band")
     x, z, y = lax.div(me, 64), lax.rem(lax.div(me, 8), 8), lax.rem(me, 8)
     at_x = [lax.rem(x + d, 2) * (64 * BANDS) + band for d in range(2)]
@@ -74,15 +84,33 @@
     following = me * BANDS + lax.rem(band + 1, BANDS)
     previous = me * BANDS + lax.rem(band + BANDS - 1, BANDS)
 
-    load_own = pltpu.make_async_copy(orb_hbm, own, load_sem.at[0])
-    load_tables = pltpu.make_async_copy(basis_hbm, tables, load_sem.at[1])
-    load_own.start()
-    load_tables.start()
-
     barrier = pltpu.get_barrier_semaphore()
     for _, device in peers:
         pl.semaphore_signal(barrier, inc=1, device_id=device, device_id_type=LOGICAL)
     pl.semaphore_signal(barrier, inc=1, device_id=previous, device_id_type=LOGICAL)
+
+    flat_peers = [(lax.rem(x + dx, 2) * 64 + lax.rem(y + dy, 8), at_x[dx] + at_y[dy]) for dx, dy in plane_offsets()]
+
+    def returns(source, target, number, planes):
+        first, rows = CHUNKS[number % 2]
+        for plane in planes:
+            for index, (slab, device) in enumerate(flat_peers):
+                copy = pltpu.make_async_remote_copy(
+                    src_ref=source.at[slab + plane * 8, pl.ds(first, rows)],
+                    dst_ref=target.at[me, pl.ds(first, rows)],
+                    send_sem=send_sem.at[number],
+                    recv_sem=recv_sem.at[number],
+                    device_id=device + plane * (8 * BANDS),
+                    device_id_type=LOGICAL,
+                )
+                if index == len(flat_peers) - 1:
+                    pl.when(z != plane)(copy.start)
+                else:
+                    copy.start()
+
+    def keep(source, target, number):
+        first, rows = CHUNKS[number % 2]
+        target[me, pl.ds(first, rows)] = source[me, pl.ds(first, rows)]
 
     def sends(source, target, number):
         first, rows = CHUNKS[number % 2]
@@ -166,14 +194,15 @@
     for chunk in range(2):
         whole(out1, in1, chunk).wait_recv()
         middle(chunk)
-        sends(out2, in2, 2 + chunk)
+        keep(out2, in2, 2 + chunk)
+        returns(out2, in2, 2 + chunk, range(8))
     whole(out2, in2, 2).wait_recv()
     field = backward(0)
     own_part = [field[0] * own[0] + field[1] * own[1], field[1] * own[0] + field[2] * own[1]]
     whole(out2, in2, 3).wait_recv()
     field = backward(1)
-    out_ref[0] = -(own_part[0] + (field[0] * other[0] + field[1] * other[1]))
-    out_ref[1] = -(own_part[1] + (field[2] * other[0] + field[3] * other[1]))
+    out_ref[0] = (own_part[0] + (field[0] * other[0] + field[1] * other[1]))
+    out_ref[1] = (own_part[1] + (field[2] * other[0] + field[3] * other[1]))
     shift.wait_send()
     for number in range(4):
         source, target = ((out1, in1), (out2, in2))[number // 2]
@@ -185,8 +214,8 @@
     pair = pltpu.VMEM((2, N, N), jnp.float32)
     result = pl.pallas_call(
         kernel,
-        out_shape=jax.ShapeDtypeStruct((2, N, N), jnp.float32),
-        in_specs=[pl.BlockSpec(memory_space=pl.ANY)] * 2,
+        out_shape=pltpu.VMEM((2, N, N), jnp.float32),
+        in_specs=[pl.BlockSpec(memory_space=pltpu.HBM)] * 2,
         out_specs=pl.BlockSpec(memory_space=pltpu.VMEM),
         scratch_shapes=[
             pair,
@@ -206,7 +235,7 @@
         compiler_params=pltpu.CompilerParams(collective_id=0, has_side_effects=True),
         name="exchange",
     )(orbitals.reshape(2, N, N), jnp.asarray(basis()))
-    return result.reshape(orbitals.shape)
+    return -result.reshape(orbitals.shape)
 
 
 def solution(mesh):

time: 43.9 us -> 41.3 us (0.941)
  the two profiles are of different devices: /device:TPU:12 before, /device:TPU:8 now
where the time goes in v2:
time: 41.3 us; the launch traced here: 41.2 us
  Pallas kernels  40.5 us (98%)
  other arithmetic  0.67 us (2%)
    pallas_call x1, Pallas kernels, body(): pl.pallas_call(kernel, out_shape=pltpu.VMEM((2, N, N), jnp.float32), in_s...  40.5 us

profile of v2, /device:TPU:8, one launch (start us, length us, event | category | flops | bytes accessed | tf_op | source)
XLA Modules:
  0.0 41.2 jit_solution(6613619201863539857)
XLA Ops:
  0.0 40.5 %exchange.1 = f32[2,128,128]{2,1,0:T(8,128)S(1)} custom-call(f32[2,128,128]{2,1,0:T(8,128)} %bitcast.5, bf16[4,128,128]{2,1,0:T(8,128)(2,1)} %constant.2.clone.basis_hbm), custom_call_target="tpu_custom_call" | custom-call | tf_op jit(solution)/shard_map/exchange/pallas_call | solution.py:215
  40.5 0.7 %negate_bitcast_fusion = f32[2,1,128,128]{3,2,1,0:T(8,128)} fusion(f32[2,128,128]{2,1,0:T(8,128)S(1)} %exchange.1), kind=kLoop, calls=%fused_computation | loop fusion | flops 32768 | bytes 262144 | tf_op jit(solution)/shard_map/neg | solution.py:238

commit v3 on v2

--- a/solution.py
+++ b/solution.py
@@ -26,13 +26,6 @@
     high = table.astype(np.float32).astype(jnp.bfloat16)
     low = (table - high.astype(np.float64)).astype(np.float32).astype(jnp.bfloat16)
     return np.stack([high, low, high.T, low.T])
-
-
-def offsets():
-    ring = lambda d: min(d, 8 - d)
-    steps = [(dx, dz, dy) for dx in range(2) for dz in range(8) for dy in range(8)]
-    steps.remove((0, 0, 0))
-    return sorted(steps, key=lambda s: -(s[0] + ring(s[1]) + ring(s[2])))
 
 
 def plane_offsets():
@@ -78,52 +71,56 @@
     me, band = lax.axis_index("slab"), lax.axis_index("band")
     x, z, y = lax.div(me, 64), lax.rem(lax.div(me, 8), 8), lax.rem(me, 8)
     at_x = [lax.rem(x + d, 2) * (64 * BANDS) + band for d in range(2)]
-    at_z = [lax.rem(z + d, 8) * (8 * BANDS) for d in range(8)]
     at_y = [lax.rem(y + d, 8) * BANDS for d in range(8)]
-    peers = [(lax.rem(x + dx, 2) * 64 + lax.rem(z + dz, 8) * 8 + lax.rem(y + dy, 8), at_x[dx] + at_z[dz] + at_y[dy]) for dx, dz, dy in offsets()]
     following = me * BANDS + lax.rem(band + 1, BANDS)
     previous = me * BANDS + lax.rem(band + BANDS - 1, BANDS)
-
-    barrier = pltpu.get_barrier_semaphore()
-    for _, device in peers:
-        pl.semaphore_signal(barrier, inc=1, device_id=device, device_id_type=LOGICAL)
-    pl.semaphore_signal(barrier, inc=1, device_id=previous, device_id_type=LOGICAL)
-
-    flat_peers = [(lax.rem(x + dx, 2) * 64 + lax.rem(y + dy, 8), at_x[dx] + at_y[dy]) for dx, dy in plane_offsets()]
-
-    def returns(source, target, number, planes):
-        first, rows = CHUNKS[number % 2]
-        for plane in planes:
-            for index, (slab, device) in enumerate(flat_peers):
-                copy = pltpu.make_async_remote_copy(
-                    src_ref=source.at[slab + plane * 8, pl.ds(first, rows)],
-                    dst_ref=target.at[me, pl.ds(first, rows)],
-                    send_sem=send_sem.at[number],
-                    recv_sem=recv_sem.at[number],
-                    device_id=device + plane * (8 * BANDS),
-                    device_id_type=LOGICAL,
-                )
-                if index == len(flat_peers) - 1:
-                    pl.when(z != plane)(copy.start)
-                else:
-                    copy.start()
 
     def keep(source, target, number):
         first, rows = CHUNKS[number % 2]
         target[me, pl.ds(first, rows)] = source[me, pl.ds(first, rows)]
 
+    flat = [(lax.rem(x + dx, 2) * 64 + lax.rem(y + dy, 8), at_x[dx] + at_y[dy]) for dx, dy in plane_offsets()]
+    at_z = [lax.rem(z + d, 8) for d in range(8)]
+    rounds = [[at_z[step] for step in steps] for steps in ((4,), (3, 5), (2, 6), (1, 7), (0,))]
+
+    def peers():
+        for planes in rounds:
+            for slab, device in flat[:-1] if planes is rounds[-1] else flat:
+                for plane in planes:
+                    yield slab + plane * 8, device + plane * (8 * BANDS)
+
+    def copy_to(source, target, number, slab, device):
+        first, rows = CHUNKS[number % 2]
+        return pltpu.make_async_remote_copy(
+            src_ref=source.at[slab, pl.ds(first, rows)],
+            dst_ref=target.at[me, pl.ds(first, rows)],
+            send_sem=send_sem.at[number],
+            recv_sem=recv_sem.at[number],
+            device_id=device,
+            device_id_type=LOGICAL,
+        )
+
     def sends(source, target, number):
-        first, rows = CHUNKS[number % 2]
-        for slab, device in peers:
-            pltpu.make_async_remote_copy(
-                src_ref=source.at[slab, pl.ds(first, rows)],
-                dst_ref=target.at[me, pl.ds(first, rows)],
-                send_sem=send_sem.at[number],
-                recv_sem=recv_sem.at[number],
-                device_id=device,
-                device_id_type=LOGICAL,
-            ).start()
-        target[me, pl.ds(first, rows)] = source[me, pl.ds(first, rows)]
+        for slab, device in peers():
+            copy_to(source, target, number, slab, device).start()
+        keep(source, target, number)
+
+    def returns(source, target, number):
+        for plane in range(8):
+            for row in (0, 1, 2, 7, 3, 6, 4, 5):
+                for step in (1, 0):
+                    slab = lax.rem(x + step, 2) * 64 + plane * 8 + row
+                    out_copy = copy_to(source, target, number, slab, at_x[step] + (plane * 8 + row) * BANDS)
+                    if step == 1:
+                        out_copy.start()
+                    else:
+                        pl.when(slab != me)(out_copy.start)
+        keep(source, target, number)
+
+    barrier = pltpu.get_barrier_semaphore()
+    for _, device in peers():
+        pl.semaphore_signal(barrier, inc=1, device_id=device, device_id_type=LOGICAL)
+    pl.semaphore_signal(barrier, inc=1, device_id=previous, device_id_type=LOGICAL)
 
     def whole(source, target, number):
         first, rows = CHUNKS[number % 2]
@@ -194,8 +191,7 @@
     for chunk in range(2):
         whole(out1, in1, chunk).wait_recv()
         middle(chunk)
-        keep(out2, in2, 2 + chunk)
-        returns(out2, in2, 2 + chunk, range(8))
+        returns(out2, in2, 2 + chunk)
     whole(out2, in2, 2).wait_recv()
     field = backward(0)
     own_part = [field[0] * own[0] + field[1] * own[1], field[1] * own[0] + field[2] * own[1]]

time: 41.3 us -> 41.1 us (level)
  the two profiles are of different devices: /device:TPU:8 before, /device:TPU:2 now
where the time goes in v3:
time: 41.1 us; the launch traced here: 41 us
  Pallas kernels  40.3 us (98%)
  other arithmetic  0.67 us (2%)
    pallas_call x1, Pallas kernels, body(): pl.pallas_call(kernel, out_shape=pltpu.VMEM((2, N, N), jnp.float32), in_s...  40.3 us

profile of v3, /device:TPU:2, one launch (start us, length us, event | category | flops | bytes accessed | tf_op | source)
XLA Modules:
  0.0 41.0 jit_solution(14691617096692453637)
XLA Ops:
  0.0 40.3 %exchange.1 = f32[2,128,128]{2,1,0:T(8,128)S(1)} custom-call(f32[2,128,128]{2,1,0:T(8,128)} %bitcast.5, bf16[4,128,128]{2,1,0:T(8,128)(2,1)} %constant.2.clone.basis_hbm), custom_call_target="tpu_custom_call" | custom-call | tf_op jit(solution)/shard_map/exchange/pallas_call | solution.py:211
  40.3 0.7 %negate_bitcast_fusion = f32[2,1,128,128]{3,2,1,0:T(8,128)} fusion(f32[2,128,128]{2,1,0:T(8,128)S(1)} %exchange.1), kind=kLoop, calls=%fused_computation | loop fusion | flops 32768 | bytes 262144 | tf_op jit(solution)/shard_map/neg | solution.py:234
